TPU v7x, 32 devices: a whole 2x2x4 slice. The times are simulated.
32 devices in a mesh: node: 4 (over y, x), intra: 8 (over z, core).
Axes of the slice: x: 2, y: 2, z: 4, core: 2. Of those that a mesh axis runs over, the one named last changes fastest.
Arguments:
- gradients: bfloat16 [4, 8, 3072, 512], P('node', 'intra'), as said below
- sign_table: int32 [64, 512], replicated, may hold values from -1 to 1, as said below
- loss_scale: float32 [1], replicated, may hold values from 256 to 65536
- step_count: int32 [1], replicated, may hold values from 1 to 8
- weights: float32 [3072, 512], P('intra', 'node'), may hold values from -6 to 6
- first_moment: float32 [3072, 512], P('intra', 'node'), may hold values from -3 to 3
- second_moment: float32 [3072, 512], P('intra', 'node'), may hold values from 0.01 to 0.1
Outputs:
- new_weights: float32 [3072, 512], P('intra', 'node')
- new_first: float32 [3072, 512], P('intra', 'node')
- new_second: float32 [3072, 512], P('intra', 'node')
Inputs may be any that keep to these rules, and one draw needn't show every extreme that they name: `gradients`: each replica's gradient is multiplied by loss_scale. `sign_table`: every entry is -1 or 1.
All inputs are finite; a program needn't handle non-finite values.
Results may differ from a plain program's by a relative error of at most 0.0003.
Values sent between devices are 32-bit elements; how exact they have to be, the bound alone decides.
A program may use at most 128 MiB of HBM per device.

v0:
```python
import math

import jax
import jax.numpy as jnp
from jax import lax
from jax.sharding import PartitionSpec as P

BLOCK = 128
SIGN_ROWS = 64


def hadamard(order):
    index = jnp.arange(order, dtype=jnp.int32)
    common = index[:, None] & index[None, :]
    parity = jnp.zeros((order, order), jnp.int32)
    for bit_index in range(order.bit_length() - 1):
        parity = parity ^ common >> bit_index & 1
    return 1 - 2 * parity


def shards(gradients, sign_table, loss_scale, step_count, weights, first_moment, second_moment):
    local_grad = gradients[0, 0]
    row_count, col_count = local_grad.shape
    owned_rows = weights.shape[0]
    table_int = hadamard(BLOCK)
    table_half = table_int.astype(jnp.bfloat16)
    table_full = table_int.astype(jnp.float32)
    inverse_root = 1.0 / math.sqrt(BLOCK)
    sign_half = sign_table.astype(jnp.bfloat16)
    repeats = local_grad.shape[0] // SIGN_ROWS
    signed = (local_grad * jnp.tile(sign_half, (repeats, 1))).reshape(-1, BLOCK)
    spun = jnp.dot(signed, table_half, preferred_element_type=jnp.float32) * inverse_root
    rotated = spun.reshape(local_grad.shape[0], col_count)
    local_top = jnp.max(jnp.abs(rotated))
    top_value = lax.pmax(local_top, ("node", "intra"))
    level_scale = 127.0 / top_value
    spun = rotated
    partial_value = lax.psum_scatter(
        jnp.floor(spun * level_scale + 0.5), "intra", scatter_dimension=0, tiled=True
    )
    summed = lax.psum_scatter(partial_value, "node", scatter_dimension=1, tiled=True)
    replicas = lax.axis_size("node") * lax.axis_size("intra")
    factor = top_value / (127.0 * replicas * loss_scale[0])
    scaled = summed * factor
    back = jnp.dot(scaled, table_full, precision=lax.Precision.HIGHEST) * inverse_root
    column_start = lax.axis_index("node") * BLOCK
    own_signs = lax.dynamic_slice_in_dim(sign_table, column_start, BLOCK, 1)
    own_tile = jnp.tile(own_signs, (owned_rows // SIGN_ROWS, 1)).astype(jnp.float32)
    grad = back * own_tile
    new_first = 0.9 * first_moment + 0.1 * grad
    new_second = 0.95 * second_moment + 0.05 * grad * grad
    steps_float = step_count[0].astype(jnp.float32)
    first_hat = new_first / (1.0 - jnp.power(jnp.float32(0.9), steps_float))
    second_hat = new_second / (1.0 - jnp.power(jnp.float32(0.95), steps_float))
    update = first_hat / (jnp.sqrt(second_hat) + 1e-08) + 0.1 * weights
    new_weights = weights - 0.2 * update
    return (new_weights, new_first, new_second)


def solution(mesh):
    placed = (
        P("node", "intra", None, None),
        P(),
        P(),
        P(),
        P("intra", "node"),
        P("intra", "node"),
        P("intra", "node"),
    )
    return jax.shard_map(
        shards,
        mesh=mesh,
        in_specs=placed,
        out_specs=(P("intra", "node"), P("intra", "node"), P("intra", "node")),
        check_vma=False,
    )
```

profile of v0, /device:TPU:0, one launch (start us, length us, event | category | flops | bytes accessed | tf_op | source)
XLA Modules:
  0.0 188.5 jit_solution(14757925594559868507)
XLA Ops:
  7.2 0.0 reduce-scatter.3.cloned.1.call-start
  7.2 0.9 convert_element_type.20
  8.1 2.0 %tile.6 = bf16[48,64,1,512]{3,1,0,2:T(8,128)(2,1)} broadcast(bf16[64,512]{1,0:T(8,128)(2,1)S(1)} %convert_element_type.20), dimensions={1,3} | broadcast | bytes 3211264 | tf_op jit(solution)/shard_map/tile | solution.py:31
  10.2 4.5 %tile.7 = bf16[12288,128]{1,0:T(8,128)(2,1)S(1)} reshape(bf16[48,64,1,512]{3,1,0,2:T(8,128)(2,1)} %tile.6) | data formatting | bytes 6291456 | tf_op jit(solution)/shard_map/tile | solution.py:31
  14.7 6.0 %squeeze.2 = bf16[12288,128]{1,0:T(8,128)(2,1)} reshape(bf16[1,1,3072,512]{3,2,1,0:T(8,128)(2,1)} %param.7) | data formatting | bytes 6291456 | tf_op jit(solution)/shard_map/squeeze | solution.py:22
  20.7 6.4 %abs_reduce_fusion = (f32[]{:T(128)}, f32[12288,128]{1,0:T(8,128)}) fusion(bf16[12288,128]{1,0:T(8,128)(2,1)} %squeeze.2, bf16[12288,128]{1,0:T(8,128)(2,1)S(1)} %tile.7), kind=kOutput, calls=%fused_computation.1 | convolution fusion | flops 409337856 | bytes 12582916 | tf_op jit(solution)/shard_map/dot_general | solution.py:32
  27.1 42.2 %pmax.7 = f32[]{:T(128)} all-reduce(f32[]{:T(128)} %get-tuple-element.6), channel_id=1, replica_groups=mesh['node'=4,'intra'=8] {'node','intra'}, use_global_device_ids=true, to_apply=%region_1.0 | all-reduce | flops 1 | bytes 8 | tf_op jit(solution)/shard_map/pmax | solution.py:35
  69.9 4.9 %add_floor_fusion = f32[12288,128]{1,0:T(8,128)} fusion(f32[12288,128]{1,0:T(8,128)} %get-tuple-element.7, f32[]{:T(128)S(6)} %mul.81), kind=kLoop, calls=%fused_computation | loop fusion | flops 4718592 | bytes 12582916 | tf_op jit(solution)/shard_map/floor | solution.py:39
  74.8 7.1 %floor.7 = f32[3072,512]{1,0:T(8,128)} reshape(f32[12288,128]{1,0:T(8,128)} %add_floor_fusion) | data formatting | bytes 12582912 | tf_op jit(solution)/shard_map/floor | solution.py:39
  81.9 0.0 copy-start
  81.9 0.0 copy-start.1
  81.9 0.0 copy-start.2
  81.9 0.0 reduce-scatter.3.cloned.1.call-update
  82.0 0.0 reduce-scatter.5.cloned.1.call-start
  82.0 69.8 %reduce-scatter.3.cloned.1.call-done = f32[384,512]{1,0:T(8,128)} async-done(((f32[3072,512]{1,0:T(8,128)}), f32[384,512]{1,0:T(8,128)}) %reduce-scatter.3.cloned.1.call-update) | async-done | bytes 786448 | tf_op jit(solution)/shard_map/reduce_scatter | solution.py:38
  151.8 0.0 reduce-scatter.5.cloned.1.call-update
  153.9 0.8 dynamic-slice_convert_fusion
  154.7 24.7 %reduce-scatter.5.cloned.1.call-done = f32[384,128]{1,0:T(8,128)} async-done(((f32[384,512]{1,0:T(8,128)}), f32[384,128]{1,0:T(8,128)}) %reduce-scatter.5.cloned.1.call-update) | async-done | bytes 196624 | tf_op jit(solution)/shard_map/reduce_scatter | solution.py:41
  179.4 0.0 copy-done
  179.4 0.0 copy-done.1
  179.4 0.0 copy-done.2
  179.4 2.2 %multiply_subtract_fusion = (f32[384,128]{1,0:T(8,128)}, f32[384,128]{1,0:T(8,128)}, f32[384,128]{1,0:T(8,128)}) fusion(f32[384,128]{1,0:T(8,128)S(1)} %copy-done, f32[]{:T(128)} %bitcast.3, f32[]{:T(128)} %bitcast.2, f32[384,128]{1,0:T(8,128)S(1)} %copy-done.1, f32[384,128]{1,0:T(8,128)S(1)} %copy-done.2, f32[384,128]{1,0:T(8,128)S(1)} %bitcast.10, ...), kind=kOutput, calls=%fused_computation.8 | convolution fusion | flops 76775424 | bytes 1572876 | tf_op jit(solution)/shard_map/dot_general | solution.py:45
  (1 shorter events, 0.0 us)
Async XLA Ops:
  7.2 144.7 %reduce-scatter.3.cloned.1.call-start = ((), (), s32[]{:S(2)}) async-start(), calls=%async_computation.2 | async-start | bytes 7077888 | tf_op jit(solution)/shard_map/reduce_scatter | solution.py:38
  81.9 97.5 %copy-start = (f32[384,128]{1,0:T(8,128)S(1)}, f32[384,128]{1,0:T(8,128)}, u32[]{:S(2)}) copy-start(f32[384,128]{1,0:T(8,128)} %param.11) | copy-start | bytes 589828
  81.9 97.5 %copy-start.1 = (f32[384,128]{1,0:T(8,128)S(1)}, f32[384,128]{1,0:T(8,128)}, u32[]{:S(2)}) copy-start(f32[384,128]{1,0:T(8,128)} %param.13) | copy-start | bytes 589828
  81.9 97.5 %copy-start.2 = (f32[384,128]{1,0:T(8,128)S(1)}, f32[384,128]{1,0:T(8,128)}, u32[]{:S(2)}) copy-start(f32[384,128]{1,0:T(8,128)} %param.12) | copy-start | bytes 589828
  82.0 97.4 %reduce-scatter.5.cloned.1.call-start = ((), (), s32[]{:S(2)}) async-start(), calls=%async_computation.3 | async-start | bytes 983040 | tf_op jit(solution)/shard_map/reduce_scatter | solution.py:41
Sparse Core Ops, SparseCore 0:
  82.1 69.7 reduce-scatter.2
  154.7 24.6 reduce-scatter.4
where the time goes:
time: 189 us; the launch traced here: 188 us
  waiting for transfers between devices  94.6 us (50%)
  blocking collectives  42.2 us (22%)
  local copies, waits for them, and re-layouts  19.7 us (10%)
  between operations  16.8 us (9%)
  matrix products  8.61 us (5%)
  other arithmetic  6.54 us (3%)
    reduce_scatter x1, waiting for transfers between devices, shards(): lax.psum_scatter(jnp.floor(spun * level_scale + 0.5), 'intra', scatter_di...  69.8 us
    pmax x1, blocking collectives, shards(): top_value = lax.pmax(local_top, ('node', 'intra'))  42.2 us
    reduce_scatter x1, waiting for transfers between devices, shards(): lax.psum_scatter(partial_value, 'node', scatter_dimension=1, tiled=True)  24.7 us
    floor x1, local copies, waits for them, and re-layouts, shards(): jnp.floor(spun * level_scale + 0.5)  7.15 us
    another operation x2, local copies, waits for them, and re-layouts, shards(): signed = (local_grad * jnp.tile(sign_half, (repeats, 1))).reshape(-1, BLOCK)  6.53 us
    dot_general x1, matrix products, shards(): jnp.dot(signed, table_half, preferred_element_type=jnp.float32)  6.38 us
    squeeze x1, local copies, waits for them, and re-layouts, shards(): local_grad = gradients[0, 0]  6.02 us
    floor x1, other arithmetic, shards(): jnp.floor(spun * level_scale + 0.5)  4.86 us
  transfers between devices with their start and end apart: 2, of which 2 were waited for; matrix products, arithmetic and copies ran while one was open for 0% of the time, Pallas kernels for 0%

commit v1 on v0

v1 whole, which is shorter than its diff:
```python
import functools
import math

import jax
import jax.numpy as jnp
from jax import lax
from jax.experimental import pallas as pl
from jax.experimental.pallas import tpu as pltpu
from jax.sharding import PartitionSpec as P

BLOCK = 128
SIGN_ROWS = 64
CORES = 2
SLOTS = 4
ROOT = 1.0 / math.sqrt(BLOCK)
MESH = pl.DeviceIdType.MESH


def hadamard(order):
    index = jnp.arange(order, dtype=jnp.int32)
    common = index[:, None] & index[None, :]
    parity = jnp.zeros((order, order), jnp.int32)
    for bit_index in range(order.bit_length() - 1):
        parity = parity ^ common >> bit_index & 1
    return 1 - 2 * parity


def reduce_kernel(
    n_node, n_intra, grad_ref, sign_ref, table_ref, sum_ref, top_ref,
    stage, lev, pair, first, second, up, down, peak, near, far,
    load_sem, pair_send, pair_recv, first_send, first_recv, second_send, second_recv,
    up_send, up_recv, down_send, down_recv, near_send, near_recv, far_send, far_recv,
):
    lo_count = 2
    n_z = n_intra // CORES
    owned = lev.shape[4] * 2
    node, intra = lax.axis_index("node"), lax.axis_index("intra")
    z, core = intra // CORES, intra % CORES
    hi, lo = node // lo_count, node % lo_count
    group = n_node * CORES
    me = node * CORES + core

    def at(node_index, z_index, core_index):
        return (node_index, z_index * CORES + core_index)

    def load(i):
        slot = lax.rem(i, SLOTS)
        return pltpu.make_async_copy(
            grad_ref.at[pl.ds(i * owned, owned)], stage.at[slot], load_sem.at[slot]
        )

    for i in range(min(SLOTS, n_intra)):
        load(i).start()

    barrier = pltpu.get_barrier_semaphore()
    for step in range(1, group):
        other = lax.rem(me + step, group)
        pl.semaphore_signal(
            barrier, inc=1, device_id=at(other // CORES, z, other % CORES), device_id_type=MESH
        )
    for step in range(1, n_z):
        pl.semaphore_signal(
            barrier, inc=1, device_id=at(node, lax.rem(z + step, n_z), core), device_id_type=MESH
        )

    table = table_ref[...]
    signs = sign_ref[...].astype(jnp.float32).astype(jnp.bfloat16)
    half = owned // 2

    def rotate(i, most):
        load(i).wait()
        block = stage[lax.rem(i, SLOTS)]
        for j in range(n_node):
            cols = slice(j * BLOCK, (j + 1) * BLOCK)
            part = block[:, cols].reshape(owned // SIGN_ROWS, SIGN_ROWS, BLOCK)
            signed = (part * signs[:, cols][None]).reshape(owned, BLOCK)
            spun = jnp.dot(signed, table, preferred_element_type=jnp.float32) * ROOT
            for h in range(2):
                lev[i, j // lo_count, j % lo_count, h] = spun[h * half : (h + 1) * half]
            most = jnp.maximum(most, jnp.max(jnp.abs(spun).reshape(owned // 8, 8, BLOCK), axis=0))

        @pl.when(i + SLOTS < n_intra)
        def _():
            load(i + SLOTS).start()

        return most

    most = lax.fori_loop(0, n_intra, rotate, jnp.zeros((8, BLOCK), jnp.float32))

    pl.semaphore_wait(barrier, group - 1 + n_z - 1)

    def near_copy(target, slot):
        return pltpu.make_async_remote_copy(
            src_ref=peak.at[0], dst_ref=near.at[slot], send_sem=near_send.at[target],
            recv_sem=near_recv.at[slot], device_id=at(target // CORES, z, target % CORES),
            device_id_type=MESH,
        )

    def far_copy(target, slot):
        return pltpu.make_async_remote_copy(
            src_ref=peak.at[1], dst_ref=far.at[slot], send_sem=far_send.at[target],
            recv_sem=far_recv.at[slot], device_id=at(node, target, core), device_id_type=MESH,
        )

    peak[0] = most
    for step in range(1, group):
        near_copy(lax.rem(me + step, group), me).start()
    for step in range(1, group):
        other = lax.rem(me + step, group)
        near_copy(other, other).wait_recv()
        most = jnp.maximum(most, near[other])
    peak[1] = most
    for step in range(1, n_z):
        far_copy(lax.rem(z + step, n_z), z).start()
    for step in range(1, n_z):
        other = lax.rem(z + step, n_z)
        far_copy(other, other).wait_recv()
        most = jnp.maximum(most, far[other])
    top_value = jnp.max(jnp.max(most, axis=0, keepdims=True), axis=1, keepdims=True)
    top_ref[...] = jnp.broadcast_to(top_value, (8, BLOCK))
    level_scale = 127.0 / top_value

    def piece(k):
        last = n_z - 1
        lower = jnp.where(k < last - z, last - k, k - (last - z))
        upper = jnp.where(k < z, k, last - (k - z))
        return jnp.where(z < n_z // 2, lower, upper)

    def pair_copy(p):
        return pltpu.make_async_remote_copy(
            src_ref=lev.at[p * CORES + 1 - core], dst_ref=pair.at[p], send_sem=pair_send.at[p],
            recv_sem=pair_recv.at[p], device_id=at(node, z, 1 - core), device_id_type=MESH,
        )

    lo_peer = hi * lo_count + 1 - lo
    hi_peer = (1 - hi) * lo_count + lo

    def first_copies(p):
        i = p * CORES + core
        return [
            pltpu.make_async_remote_copy(
                src_ref=src, dst_ref=first.at[p, h], send_sem=first_send.at[h, p],
                recv_sem=first_recv.at[h, p], device_id=at(peer, z, core), device_id_type=MESH,
            )
            for h, src, peer in (
                (0, lev.at[i, :, 1 - lo, 0], lo_peer),
                (1, lev.at[i, 1 - hi, :, 1], hi_peer),
            )
        ]

    def second_copies(p):
        i = p * CORES + core
        return [
            pltpu.make_async_remote_copy(
                src_ref=src, dst_ref=second.at[p, h], send_sem=second_send.at[h, p],
                recv_sem=second_recv.at[h, p], device_id=at(peer, z, core), device_id_type=MESH,
            )
            for h, src, peer in (
                (0, lev.at[i, 1 - hi, lo, 0], hi_peer),
                (1, lev.at[i, hi, 1 - lo, 1], lo_peer),
            )
        ]

    def up_copy(p):
        return pltpu.make_async_remote_copy(
            src_ref=lev.at[p * CORES + core, hi, lo], dst_ref=up.at[p], send_sem=up_send.at[p],
            recv_sem=up_recv.at[p], device_id=at(node, lax.rem(z + 1, n_z), core),
            device_id_type=MESH,
        )

    def down_copy(p):
        return pltpu.make_async_remote_copy(
            src_ref=lev.at[p * CORES + core, hi, lo], dst_ref=down.at[p], send_sem=down_send.at[p],
            recv_sem=down_recv.at[p], device_id=at(node, lax.rem(z + n_z - 1, n_z), core),
            device_id_type=MESH,
        )

    def pipeline(t, carry):
        @pl.when(t < n_z)
        def _():
            p = piece(t)
            for c in range(CORES):
                i = p * CORES + lax.rem(core + 1 + c, CORES)
                for j in range(n_node):
                    for h in range(2):
                        spot = (i, j // lo_count, j % lo_count, h)
                        lev[spot] = jnp.floor(lev[spot] * level_scale + 0.5)
                if c == 0:
                    pair_copy(p).start()

        @pl.when((t >= 1) & (t < n_z + 1))
        def _():
            p = piece(t - 1)
            i = p * CORES + core
            pair_copy(p).wait_recv()
            for j in range(n_node):
                for h in range(2):
                    spot = (j // lo_count, j % lo_count, h)
                    lev[(i,) + spot] = lev[(i,) + spot] + pair[(p,) + spot]
            for copy in first_copies(p):
                copy.start()

        @pl.when((t >= 2) & (t < n_z + 2))
        def _():
            p = piece(t - 2)
            i = p * CORES + core
            for copy in first_copies(p):
                copy.wait_recv()
            for j in range(2):
                lev[i, j, lo, 0] = lev[i, j, lo, 0] + first[p, 0, j]
                lev[i, hi, j, 1] = lev[i, hi, j, 1] + first[p, 1, j]
            for copy in second_copies(p):
                copy.start()

        @pl.when(t >= 3)
        def _():
            p = piece(t - 3)
            i = p * CORES + core
            for copy in second_copies(p):
                copy.wait_recv()
            for h in range(2):
                lev[i, hi, lo, h] = lev[i, hi, lo, h] + second[p, h]

            @pl.when((p >= z) & (z > 0))
            def _():
                up_copy(p).wait_recv()
                lev[i, hi, lo] = lev[i, hi, lo] + up[p]

            @pl.when((p <= z) & (z < n_z - 1))
            def _():
                down_copy(p).wait_recv()
                lev[i, hi, lo] = lev[i, hi, lo] + down[p]

            @pl.when(p > z)
            def _():
                up_copy(p).start()

            @pl.when(p < z)
            def _():
                down_copy(p).start()

        return carry

    lax.fori_loop(0, n_z + 3, pipeline, 0)

    for h in range(2):
        sum_ref[h * half : (h + 1) * half, :] = lev[intra, hi, lo, h]

    for step in range(1, group):
        near_copy(lax.rem(me + step, group), me).wait_send()
    for step in range(1, n_z):
        far_copy(lax.rem(z + step, n_z), z).wait_send()

    def finish(p, carry):
        pair_copy(p).wait_send()
        for copy in first_copies(p) + second_copies(p):
            copy.wait_send()

        @pl.when(p > z)
        def _():
            up_copy(p).wait_send()

        @pl.when(p < z)
        def _():
            down_copy(p).wait_send()

        return carry

    lax.fori_loop(0, n_z, finish, 0)


def adam_kernel(
    replicas, sum_ref, top_ref, sign_ref, table_ref, scale_ref, step_ref,
    weight_ref, first_ref, second_ref, new_weight_ref, new_first_ref, new_second_ref,
):
    owned = sum_ref.shape[0]
    table = table_ref[...]
    summed = sum_ref[...]
    high = jnp.floor(summed * (1.0 / 64.0))
    low = summed - high * 64.0
    back = jnp.dot(high.astype(jnp.bfloat16), table, preferred_element_type=jnp.float32) * 64.0
    back = back + jnp.dot(low.astype(jnp.bfloat16), table, preferred_element_type=jnp.float32)
    ones = jnp.ones((1, BLOCK), jnp.float32)
    factor = top_ref[0:1, :] / (ones * (127.0 * replicas * scale_ref[0]))
    signs = sign_ref[...].astype(jnp.float32) * (factor * ROOT)
    grad = (back.reshape(owned // SIGN_ROWS, SIGN_ROWS, BLOCK) * signs[None]).reshape(owned, BLOCK)
    steps = ones * step_ref[0].astype(jnp.float32)
    first_unbias = 1.0 / (1.0 - jnp.exp(steps * math.log(0.9)))
    second_unbias = 1.0 / (1.0 - jnp.exp(steps * math.log(0.95)))
    new_first = 0.9 * first_ref[...] + 0.1 * grad
    new_second = 0.95 * second_ref[...] + 0.05 * grad * grad
    new_first_ref[...] = new_first
    new_second_ref[...] = new_second
    weights = weight_ref[...]
    update = (new_first * first_unbias) / (jnp.sqrt(new_second * second_unbias) + 1e-08)
    new_weight_ref[...] = weights - 0.2 * (update + 0.1 * weights)


def shards(gradients, sign_table, loss_scale, step_count, weights, first_moment, second_moment):
    n_node, n_intra = lax.axis_size("node"), lax.axis_size("intra")
    n_z = n_intra // CORES
    local = gradients.reshape(gradients.shape[2:])
    rows, columns = local.shape
    owned = weights.shape[0]
    half = owned // 2
    n_hi = n_node // 2
    table = hadamard(BLOCK).astype(jnp.bfloat16)
    vmem = pl.BlockSpec(memory_space=pltpu.VMEM)
    smem = pl.BlockSpec(memory_space=pltpu.SMEM)
    dma = pltpu.SemaphoreType.DMA
    group = n_node * CORES
    f32 = jnp.float32
    summed, top = pl.pallas_call(
        functools.partial(reduce_kernel, n_node, n_intra),
        out_shape=(
            jax.ShapeDtypeStruct((owned, BLOCK), f32),
            jax.ShapeDtypeStruct((8, BLOCK), f32),
        ),
        in_specs=[pl.BlockSpec(memory_space=pl.ANY), vmem, vmem],
        out_specs=(vmem, vmem),
        scratch_shapes=[
            pltpu.VMEM((SLOTS, owned, columns), jnp.bfloat16),
            pltpu.VMEM((n_intra, n_hi, 2, 2, half, BLOCK), f32),
            pltpu.VMEM((n_z, n_hi, 2, 2, half, BLOCK), f32),
            pltpu.VMEM((n_z, 2, 2, half, BLOCK), f32),
            pltpu.VMEM((n_z, 2, half, BLOCK), f32),
            pltpu.VMEM((n_z, 2, half, BLOCK), f32),
            pltpu.VMEM((n_z, 2, half, BLOCK), f32),
            pltpu.VMEM((2, 8, BLOCK), f32),
            pltpu.VMEM((group, 8, BLOCK), f32),
            pltpu.VMEM((n_z, 8, BLOCK), f32),
            dma((SLOTS,)),
            dma((n_z,)), dma((n_z,)),
            dma((2, n_z)), dma((2, n_z)),
            dma((2, n_z)), dma((2, n_z)),
            dma((n_z,)), dma((n_z,)),
            dma((n_z,)), dma((n_z,)),
            dma((group,)), dma((group,)),
            dma((n_z,)), dma((n_z,)),
        ],
        compiler_params=pltpu.CompilerParams(
            collective_id=0, has_side_effects=True, vmem_limit_bytes=60 * 1024 * 1024
        ),
    )(local, sign_table, table)
    own_signs = lax.dynamic_slice_in_dim(sign_table, lax.axis_index("node") * BLOCK, BLOCK, 1)
    shape = jax.ShapeDtypeStruct((owned, BLOCK), f32)
    return pl.pallas_call(
        functools.partial(adam_kernel, float(n_node * n_intra)),
        out_shape=(shape, shape, shape),
        in_specs=[vmem, vmem, vmem, vmem, smem, smem, vmem, vmem, vmem],
        out_specs=(vmem, vmem, vmem),
    )(summed, top, own_signs, table, loss_scale, step_count, weights, first_moment, second_moment)


def solution(mesh):
    own = P("intra", "node")
    return jax.shard_map(
        shards,
        mesh=mesh,
        in_specs=(P("node", "intra", None, None), P(), P(), P(), own, own, own),
        out_specs=(own, own, own),
        check_vma=False,
    )
```

time: 189 us -> 57.7 us (0.31)
  waiting for transfers between devices: 94.6 us -> 0 us
  Pallas kernels: 0 us -> 53.4 us
  blocking collectives: 42.2 us -> 0 us
  local copies, waits for them, and re-layouts: 19.7 us -> 1.38 us
  between operations: 16.8 us -> 1.93 us
  matrix products: 8.61 us -> 0 us
  other arithmetic: 6.54 us -> 0.68 us
    reduce_scatter x2 -> x0, waiting for transfers between devices: 94.5 us -> none  [the longest x1 69.8 us: shards(): lax.psum_scatter(jnp.floor(spun * level_scale + 0.5), 'intra', scatter_di...]
    pallas_call x0 -> x2, Pallas kernels: none -> 53.4 us  [the longest x1 51.1 us: shards(): pl.pallas_call(functools.partial(reduce_kernel, n_node, n_intra), out_sha...]
    pmax x1 -> x0, blocking collectives: 42.2 us -> none  [shards(): top_value = lax.pmax(local_top, ('node', 'intra'))]
    dot_general x2 -> x0, matrix products: 8.61 us -> none  [the longest x1 6.38 us: shards(): jnp.dot(signed, table_half, preferred_element_type=jnp.float32)]
    floor x1 -> x0, local copies, waits for them, and re-layouts: 7.15 us -> none  [shards(): jnp.floor(spun * level_scale + 0.5)]
    another operation x3 -> x0, local copies, waits for them, and re-layouts: 6.55 us -> none  [the longest x2 6.53 us: shards(): signed = (local_grad * jnp.tile(sign_half, (repeats, 1))).reshape(-1, BLOCK)]
    squeeze x1 -> x0, local copies, waits for them, and re-layouts: 6.02 us -> none  [shards(): local_grad = gradients[0, 0]]
    floor x1 -> x0, other arithmetic: 4.86 us -> none  [shards(): jnp.floor(spun * level_scale + 0.5)]
  transfers between devices with their start and end apart: 2 -> 0, of which waited for: 2 -> 0; matrix products, arithmetic and copies ran while one was open for 0% -> 0% of each run, Pallas kernels for 0% -> 0%
where the time goes in v1:
time: 57.7 us; the launch traced here: 57.4 us
  Pallas kernels  53.4 us (93%)
  between operations  1.93 us (3%)
  local copies, waits for them, and re-layouts  1.38 us (2%)
  other arithmetic  0.68 us (1%)
    pallas_call x1, Pallas kernels, shards(): pl.pallas_call(functools.partial(reduce_kernel, n_node, n_intra), out_sha...  51.1 us
    pallas_call x1, Pallas kernels, shards(): pl.pallas_call(functools.partial(adam_kernel, float(n_node * n_intra)), o...  2.37 us
    dynamic_slice x1, local copies, waits for them, and re-layouts, shards(): lax.dynamic_slice_in_dim(sign_table, lax.axis_index('node') * BLOCK, BLOC...  1.38 us

profile of v1, /device:TPU:0, one launch (start us, length us, event | category | flops | bytes accessed | tf_op | source)
XLA Modules:
  0.0 57.4 jit_solution(16025938193243064685)
XLA Ops:
  1.9 1.4 %constant_dynamic-slice_fusion.sign_ref = s32[64,128]{1,0:T(8,128)} fusion(s32[64,512]{1,0:T(8,128)} %sign_ref.1, s32[]{:T(128)S(6)} %select_n.3), kind=kLoop, calls=%fused_computation.1 | loop fusion | bytes 65540 | tf_op jit(solution)/shard_map/dynamic_slice | solution.py:345
  3.3 0.7 %subtract_convert_fusion.table_ref = bf16[128,128]{1,0:T(8,128)(2,1)} fusion(), kind=kLoop, calls=%fused_computation | loop fusion | flops 393216 | bytes 32768 | tf_op jit(solution)/shard_map/convert_element_type | solution.py:307
  4.0 51.1 %shard_map.94 = (f32[384,128]{1,0:T(8,128)}, f32[8,128]{1,0:T(8,128)}) custom-call(bf16[3072,512]{1,0:T(8,128)(2,1)} %bitcast.1, s32[64,512]{1,0:T(8,128)} %sign_ref.1, bf16[128,128]{1,0:T(8,128)(2,1)} %subtract_convert_fusion.table_ref), custom_call_target="tpu_custom_call" | custom-call | tf_op jit(solution)/shard_map/pallas_call | solution.py:313
  55.0 2.4 %shard_map.95 = (f32[384,128]{1,0:T(8,128)}, f32[384,128]{1,0:T(8,128)}, f32[384,128]{1,0:T(8,128)}) custom-call(f32[384,128]{1,0:T(8,128)} %get-tuple-element.5.sum_ref, f32[8,128]{1,0:T(8,128)} %get-tuple-element.6.top_ref, s32[64,128]{1,0:T(8,128)} %constant_dynamic-slice_fusion.sign_ref, bf16[128,128]{1,0:T(8,128)(2,1)} %subtract_convert_fusion.table_ref, ...), custom_call_target="tpu_custom_call" | custom-call | tf_op jit(solution)/shard_map/pallas_call | solution.py:347

commit v2 on v1

v2 whole, which is shorter than its diff:
```python
import functools
import math

import jax
import jax.numpy as jnp
from jax import lax
from jax.experimental import pallas as pl
from jax.experimental.pallas import tpu as pltpu
from jax.sharding import PartitionSpec as P

BLOCK = 128
SIGN_ROWS = 64
CORES = 2
SLOTS = 4
ROOT = 1.0 / math.sqrt(BLOCK)
MESH = pl.DeviceIdType.MESH


def hadamard_table():
    common = lax.broadcasted_iota(jnp.int32, (BLOCK, BLOCK), 0) & lax.broadcasted_iota(
        jnp.int32, (BLOCK, BLOCK), 1
    )
    parity = common
    for bit_index in range(1, BLOCK.bit_length() - 1):
        parity = parity ^ (common >> bit_index)
    return (1 - 2 * (parity & 1)).astype(jnp.float32).astype(jnp.bfloat16)


def reduce_kernel(
    n_node, n_intra, grad_ref, sign_ref, sum_ref, top_ref,
    stage, lev, pair, raw, first, second, third, peak, near, far,
    load_sem, pair_send, pair_recv, raw_send, raw_recv, first_send, first_recv,
    second_send, second_recv, third_send, third_recv, near_send, near_recv, far_send, far_recv,
):
    lo_count = 2
    n_z = n_intra // CORES
    owned = lev.shape[4] * 2
    half = owned // 2
    node, intra = lax.axis_index("node"), lax.axis_index("intra")
    z, core = intra // CORES, intra % CORES
    hi, lo = node // lo_count, node % lo_count
    group = n_node * CORES
    me = node * CORES + core

    def at(node_index, z_index, core_index):
        return (node_index, z_index * CORES + core_index)

    def send(src, dst, send_sem, recv_sem, device):
        return pltpu.make_async_remote_copy(
            src_ref=src, dst_ref=dst, send_sem=send_sem, recv_sem=recv_sem,
            device_id=device, device_id_type=MESH,
        )

    def piece(k):
        last = n_z - 1
        lower = jnp.where(k < last - z, last - k, k - (last - z))
        upper = jnp.where(k < z, k, last - (k - z))
        return jnp.where(z < n_z // 2, lower, upper)

    early = min(2, n_z)

    def block_at(q):
        other = (q >= early) & (q < early + n_z)
        k = jnp.where(q < early, q, jnp.where(other, q - early, q - n_z))
        return piece(k) * CORES + jnp.where(other, 1 - core, core)

    def load(q):
        slot = lax.rem(q, SLOTS)
        return pltpu.make_async_copy(
            grad_ref.at[pl.ds(block_at(q) * owned, owned)], stage.at[slot], load_sem.at[slot]
        )

    for q in range(min(SLOTS, n_intra)):
        load(q).start()

    barrier = pltpu.get_barrier_semaphore()
    for step in range(1, group):
        other = lax.rem(me + step, group)
        pl.semaphore_signal(
            barrier, inc=1, device_id=at(other // CORES, z, other % CORES), device_id_type=MESH
        )
    for step in range(1, n_z):
        pl.semaphore_signal(
            barrier, inc=1, device_id=at(node, lax.rem(z + step, n_z), core), device_id_type=MESH
        )

    table = hadamard_table()
    signs = sign_ref[...].astype(jnp.float32).astype(jnp.bfloat16)

    def rotate(q, most):
        load(q).wait()
        i = block_at(q)
        block = stage[lax.rem(q, SLOTS)]
        for j in range(n_node):
            cols = slice(j * BLOCK, (j + 1) * BLOCK)
            part = block[:, cols].reshape(owned // SIGN_ROWS, SIGN_ROWS, BLOCK)
            signed = (part * signs[:, cols][None]).reshape(owned, BLOCK)
            spun = jnp.dot(signed, table, preferred_element_type=jnp.float32) * ROOT
            for h in range(2):
                lev[i, j // lo_count, j % lo_count, h] = spun[h * half : (h + 1) * half]
            most = jnp.maximum(most, jnp.max(jnp.abs(spun).reshape(owned // 8, 8, BLOCK), axis=0))

        @pl.when(q + SLOTS < n_intra)
        def _():
            load(q + SLOTS).start()

        return most

    lo_peer = hi * lo_count + 1 - lo
    hi_peer = (1 - hi) * lo_count + lo

    def pair_copy(p):
        return send(
            lev.at[p * CORES + 1 - core], pair.at[p], pair_send.at[p], pair_recv.at[p],
            at(node, z, 1 - core),
        )

    def raw_copies(flip):
        target = core if flip == 0 else 1 - core
        i = piece(0) * CORES + target
        return [
            send(
                src, raw.at[flip, h], raw_send.at[flip, h], raw_recv.at[flip, h],
                at(peer, z, target),
            )
            for h, src, peer in (
                (0, lev.at[i, :, 1 - lo, 0], lo_peer),
                (1, lev.at[i, 1 - hi, :, 1], hi_peer),
            )
        ]

    def first_copies(p):
        i = p * CORES + core
        return [
            send(src, first.at[p, h], first_send.at[h, p], first_recv.at[h, p], at(peer, z, core))
            for h, src, peer in (
                (0, lev.at[i, :, 1 - lo, 0], lo_peer),
                (1, lev.at[i, 1 - hi, :, 1], hi_peer),
            )
        ]

    def second_copies(p):
        i = p * CORES + core
        return [
            send(
                src, second.at[p, h], second_send.at[h, p], second_recv.at[h, p],
                at(peer, z, core),
            )
            for h, src, peer in (
                (0, lev.at[i, 1 - hi, lo, 0], hi_peer),
                (1, lev.at[i, hi, 1 - lo, 1], lo_peer),
            )
        ]

    def third_copy(p, slot):
        return send(
            lev.at[p * CORES + core, hi, lo], third.at[slot], third_send.at[p],
            third_recv.at[slot], at(node, p, core),
        )

    def near_copy(target, slot):
        return send(
            peak.at[0], near.at[slot], near_send.at[target], near_recv.at[slot],
            at(target // CORES, z, target % CORES),
        )

    def far_copy(target, slot):
        return send(
            peak.at[1], far.at[slot], far_send.at[target], far_recv.at[slot],
            at(node, target, core),
        )

    most = lax.fori_loop(0, early, rotate, jnp.zeros((8, BLOCK), jnp.float32))
    pl.semaphore_wait(barrier, group - 1 + n_z - 1)
    for copy in raw_copies(0):
        copy.start()

    def rotate_and_send(q, most):
        most = rotate(q, most)
        pair_copy(piece(q - early)).start()
        return most

    most = lax.fori_loop(early, early + n_z, rotate_and_send, most)
    most = lax.fori_loop(early + n_z, n_intra, rotate, most)

    peak[0] = most
    for step in range(1, group):
        near_copy(lax.rem(me + step, group), me).start()
    for copy in raw_copies(1):
        copy.start()
    for step in range(1, group):
        other = lax.rem(me + step, group)
        near_copy(other, other).wait_recv()
        most = jnp.maximum(most, near[other])
    peak[1] = most
    for step in range(1, n_z):
        far_copy(lax.rem(z + step, n_z), z).start()
    for step in range(1, n_z):
        other = lax.rem(z + step, n_z)
        far_copy(other, other).wait_recv()
        most = jnp.maximum(most, far[other])
    top_value = jnp.max(jnp.max(most, axis=0, keepdims=True), axis=1, keepdims=True)
    top_ref[...] = jnp.broadcast_to(top_value, (8, BLOCK))
    level_scale = 127.0 / top_value

    def level(value):
        return jnp.floor(value * level_scale + 0.5)

    def pipeline(t, carry):
        @pl.when(t < n_z)
        def _():
            p = piece(t)
            i = p * CORES + core
            pair_copy(p).wait_recv()
            for j in range(n_node):
                for h in range(2):
                    spot = (j // lo_count, j % lo_count, h)
                    lev[(i,) + spot] = level(lev[(i,) + spot]) + level(pair[(p,) + spot])
            for copy in first_copies(p):
                copy.start()

        @pl.when(t == 1)
        def _():
            p = piece(0)
            i = p * CORES + core
            pair_copy(p).wait_recv()
            for flip in range(2):
                for copy in raw_copies(flip):
                    copy.wait_recv()

            def kept(h, j, spot):
                lev[(i,) + spot] = (
                    level(lev[(i,) + spot]) + level(pair[(p,) + spot])
                    + level(raw[0, h, j]) + level(raw[1, h, j])
                )

            for j in range(2):
                kept(0, j, (j, lo, 0))
                kept(1, j, (hi, j, 1))
            for copy in second_copies(p):
                copy.start()

        @pl.when((t >= 2) & (t <= n_z))
        def _():
            p = piece(t - 1)
            i = p * CORES + core
            for copy in first_copies(p):
                copy.wait_recv()
            for j in range(2):
                lev[i, j, lo, 0] = lev[i, j, lo, 0] + first[p, 0, j]
                lev[i, hi, j, 1] = lev[i, hi, j, 1] + first[p, 1, j]
            for copy in second_copies(p):
                copy.start()

        @pl.when(t >= 2)
        def _():
            p = piece(t - 2)
            i = p * CORES + core
            for copy in second_copies(p):
                copy.wait_recv()
            for h in range(2):
                lev[i, hi, lo, h] = lev[i, hi, lo, h] + second[p, h]

            @pl.when(p != z)
            def _():
                third_copy(p, z).start()

        return carry

    lax.fori_loop(1, n_z + 2, pipeline, 0)

    total = lev[intra, hi, lo]
    for step in range(1, n_z):
        other = lax.rem(z + step, n_z)
        third_copy(other, other).wait_recv()
        total = total + third[other]
    for h in range(2):
        sum_ref[h * half : (h + 1) * half, :] = total[h]

    for step in range(1, group):
        near_copy(lax.rem(me + step, group), me).wait_send()
    for step in range(1, n_z):
        far_copy(lax.rem(z + step, n_z), z).wait_send()
    for flip in range(2):
        for copy in raw_copies(flip):
            copy.wait_send()

    def finish(k, carry):
        p = piece(k)
        pair_copy(p).wait_send()
        for copy in second_copies(p):
            copy.wait_send()

        @pl.when(k > 0)
        def _():
            for copy in first_copies(p):
                copy.wait_send()

        @pl.when(p != z)
        def _():
            third_copy(p, z).wait_send()

        return carry

    lax.fori_loop(0, n_z, finish, 0)


def adam_kernel(
    replicas, sum_ref, top_ref, sign_ref, scale_ref, step_ref,
    weight_ref, first_ref, second_ref, new_weight_ref, new_first_ref, new_second_ref,
):
    owned = sum_ref.shape[0]
    table = hadamard_table()
    column = pl.multiple_of(lax.axis_index("node") * BLOCK, BLOCK)
    summed = sum_ref[...]
    high = jnp.floor(summed * (1.0 / 64.0))
    low = summed - high * 64.0
    back = jnp.dot(high.astype(jnp.bfloat16), table, preferred_element_type=jnp.float32) * 64.0
    back = back + jnp.dot(low.astype(jnp.bfloat16), table, preferred_element_type=jnp.float32)
    ones = jnp.ones((1, BLOCK), jnp.float32)
    factor = top_ref[0:1, :] / (ones * (127.0 * replicas * scale_ref[0]))
    signs = sign_ref[:, pl.ds(column, BLOCK)].astype(jnp.float32) * (factor * ROOT)
    grad = (back.reshape(owned // SIGN_ROWS, SIGN_ROWS, BLOCK) * signs[None]).reshape(owned, BLOCK)
    steps = ones * step_ref[0].astype(jnp.float32)
    first_unbias = 1.0 / (1.0 - jnp.exp(steps * math.log(0.9)))
    second_unbias = 1.0 / (1.0 - jnp.exp(steps * math.log(0.95)))
    new_first = 0.9 * first_ref[...] + 0.1 * grad
    new_second = 0.95 * second_ref[...] + 0.05 * grad * grad
    new_first_ref[...] = new_first
    new_second_ref[...] = new_second
    weights = weight_ref[...]
    update = (new_first * first_unbias) / (jnp.sqrt(new_second * second_unbias) + 1e-08)
    new_weight_ref[...] = weights - 0.2 * (update + 0.1 * weights)


def shards(gradients, sign_table, loss_scale, step_count, weights, first_moment, second_moment):
    n_node, n_intra = lax.axis_size("node"), lax.axis_size("intra")
    n_z = n_intra // CORES
    local = gradients.reshape(gradients.shape[2:])
    rows, columns = local.shape
    owned = weights.shape[0]
    half = owned // 2
    n_hi = n_node // 2
    vmem = pl.BlockSpec(memory_space=pltpu.VMEM)
    smem = pl.BlockSpec(memory_space=pltpu.SMEM)
    dma = pltpu.SemaphoreType.DMA
    group = n_node * CORES
    f32 = jnp.float32
    summed, top = pl.pallas_call(
        functools.partial(reduce_kernel, n_node, n_intra),
        out_shape=(
            jax.ShapeDtypeStruct((owned, BLOCK), f32),
            jax.ShapeDtypeStruct((8, BLOCK), f32),
        ),
        in_specs=[pl.BlockSpec(memory_space=pl.ANY), vmem],
        out_specs=(vmem, vmem),
        scratch_shapes=[
            pltpu.VMEM((SLOTS, owned, columns), jnp.bfloat16),
            pltpu.VMEM((n_intra, n_hi, 2, 2, half, BLOCK), f32),
            pltpu.VMEM((n_z, n_hi, 2, 2, half, BLOCK), f32),
            pltpu.VMEM((2, 2, 2, half, BLOCK), f32),
            pltpu.VMEM((n_z, 2, 2, half, BLOCK), f32),
            pltpu.VMEM((n_z, 2, half, BLOCK), f32),
            pltpu.VMEM((n_z, 2, half, BLOCK), f32),
            pltpu.VMEM((2, 8, BLOCK), f32),
            pltpu.VMEM((group, 8, BLOCK), f32),
            pltpu.VMEM((n_z, 8, BLOCK), f32),
            dma((SLOTS,)),
            dma((n_z,)), dma((n_z,)),
            dma((2, 2)), dma((2, 2)),
            dma((2, n_z)), dma((2, n_z)),
            dma((2, n_z)), dma((2, n_z)),
            dma((n_z,)), dma((n_z,)),
            dma((group,)), dma((group,)),
            dma((n_z,)), dma((n_z,)),
        ],
        compiler_params=pltpu.CompilerParams(
            collective_id=0, has_side_effects=True, vmem_limit_bytes=60 * 1024 * 1024
        ),
    )(local, sign_table)
    shape = jax.ShapeDtypeStruct((owned, BLOCK), f32)
    return pl.pallas_call(
        functools.partial(adam_kernel, float(n_node * n_intra)),
        out_shape=(shape, shape, shape),
        in_specs=[vmem, vmem, vmem, smem, smem, vmem, vmem, vmem],
        out_specs=(vmem, vmem, vmem),
    )(summed, top, sign_table, loss_scale, step_count, weights, first_moment, second_moment)


def solution(mesh):
    own = P("intra", "node")
    return jax.shard_map(
        shards,
        mesh=mesh,
        in_specs=(P("node", "intra", None, None), P(), P(), P(), own, own, own),
        out_specs=(own, own, own),
        check_vma=False,
    )
```

time: 57.7 us -> 49 us (0.85)
  Pallas kernels: 53.4 us -> 46.8 us
  local copies, waits for them, and re-layouts: 1.38 us -> 0 us
  other arithmetic: 0.68 us -> 0 us
    pallas_call x1, Pallas kernels: 51.1 us -> 44.4 us  [shards(): pl.pallas_call(functools.partial(reduce_kernel, n_node, n_intra), out_sha...]
    dynamic_slice x1 -> x0, local copies, waits for them, and re-layouts: 1.38 us -> none  [shards(): lax.dynamic_slice_in_dim(sign_table, lax.axis_index('node') * BLOCK, BLOC...]
    convert_element_type x1 -> x0, other arithmetic: 0.68 us -> none  [shards(): table = hadamard(BLOCK).astype(jnp.bfloat16)]
where the time goes in v2:
time: 49 us; the launch traced here: 48.8 us
  Pallas kernels  46.8 us (96%)
  between operations  1.93 us (4%)
    pallas_call x1, Pallas kernels, shards(): pl.pallas_call(functools.partial(reduce_kernel, n_node, n_intra), out_sha...  44.4 us
    pallas_call x1, Pallas kernels, shards(): pl.pallas_call(functools.partial(adam_kernel, float(n_node * n_intra)), o...  2.4 us

profile of v2, /device:TPU:0, one launch (start us, length us, event | category | flops | bytes accessed | tf_op | source)
XLA Modules:
  0.0 48.8 jit_solution(7234035693560394634)
XLA Ops:
  1.9 44.4 %shard_map.94 = (f32[384,128]{1,0:T(8,128)}, f32[8,128]{1,0:T(8,128)}) custom-call(bf16[3072,512]{1,0:T(8,128)(2,1)} %bitcast.1, s32[64,512]{1,0:T(8,128)} %sign_ref.3), custom_call_target="tpu_custom_call" | custom-call | tf_op jit(solution)/shard_map/pallas_call | solution.py:349
  46.4 2.4 %shard_map.95 = (f32[384,128]{1,0:T(8,128)}, f32[384,128]{1,0:T(8,128)}, f32[384,128]{1,0:T(8,128)}) custom-call(f32[384,128]{1,0:T(8,128)} %get-tuple-element.5.sum_ref, f32[8,128]{1,0:T(8,128)} %get-tuple-element.6.top_ref, s32[64,512]{1,0:T(8,128)} %sign_ref.3, f32[1]{0:T(128)S(6)} %copy.10.scale_ref, s32[1]{0:T(128)S(6)} %copy.11.step_ref, ...), custom_call_target="tpu_custom_call" | custom-call | tf_op jit(solution)/shard_map/pallas_call | solution.py:382

commit v3 on v2

--- a/solution.py
+++ b/solution.py
@@ -12,6 +12,7 @@
 SIGN_ROWS = 64
 CORES = 2
 SLOTS = 4
+SUBS = 2
 ROOT = 1.0 / math.sqrt(BLOCK)
 MESH = pl.DeviceIdType.MESH
 
@@ -129,33 +130,42 @@
             )
         ]
 
-    def first_copies(p):
-        i = p * CORES + core
-        return [
-            send(src, first.at[p, h], first_send.at[h, p], first_recv.at[h, p], at(peer, z, core))
-            for h, src, peer in (
-                (0, lev.at[i, :, 1 - lo, 0], lo_peer),
-                (1, lev.at[i, 1 - hi, :, 1], hi_peer),
-            )
-        ]
-
-    def second_copies(p):
-        i = p * CORES + core
+    part_rows = half // SUBS
+
+    def rows_of(s):
+        return pl.ds(s * part_rows, part_rows)
+
+    def first_copies(p, s):
+        i, r = p * CORES + core, rows_of(s)
         return [
             send(
-                src, second.at[p, h], second_send.at[h, p], second_recv.at[h, p],
-                at(peer, z, core),
+                src, first.at[p, h, :, r], first_send.at[h, p * SUBS + s],
+                first_recv.at[h, p * SUBS + s], at(peer, z, core),
             )
             for h, src, peer in (
-                (0, lev.at[i, 1 - hi, lo, 0], hi_peer),
-                (1, lev.at[i, hi, 1 - lo, 1], lo_peer),
+                (0, lev.at[i, :, 1 - lo, 0, r], lo_peer),
+                (1, lev.at[i, 1 - hi, :, 1, r], hi_peer),
             )
         ]
 
-    def third_copy(p, slot):
+    def second_copies(p, s):
+        i, r = p * CORES + core, rows_of(s)
+        return [
+            send(
+                src, second.at[p, h, r], second_send.at[h, p * SUBS + s],
+                second_recv.at[h, p * SUBS + s], at(peer, z, core),
+            )
+            for h, src, peer in (
+                (0, lev.at[i, 1 - hi, lo, 0, r], hi_peer),
+                (1, lev.at[i, hi, 1 - lo, 1, r], lo_peer),
+            )
+        ]
+
+    def third_copy(p, slot, s):
+        r = rows_of(s)
         return send(
-            lev.at[p * CORES + core, hi, lo], third.at[slot], third_send.at[p],
-            third_recv.at[slot], at(node, p, core),
+            lev.at[p * CORES + core, hi, lo, :, r], third.at[slot, :, r],
+            third_send.at[p * SUBS + s], third_recv.at[slot * SUBS + s], at(node, p, core),
         )
 
     def near_copy(target, slot):
@@ -206,24 +216,44 @@
     def level(value):
         return jnp.floor(value * level_scale + 0.5)
 
+    items = n_z * SUBS
+
+    def last_exchange(p, s):
+        i, r = p * CORES + core, rows_of(s)
+        for copy in second_copies(p, s):
+            copy.wait_recv()
+        for h in range(2):
+            lev[i, hi, lo, h, r] = lev[i, hi, lo, h, r] + second[p, h, r]
+
+        @pl.when(p != z)
+        def _():
+            third_copy(p, z, s).start()
+
     def pipeline(t, carry):
-        @pl.when(t < n_z)
-        def _():
-            p = piece(t)
-            i = p * CORES + core
-            pair_copy(p).wait_recv()
+        @pl.when(t == SUBS)
+        def _():
+            pair_copy(piece(0)).wait_recv()
+
+        @pl.when(t < items)
+        def _():
+            p, s = piece(t // SUBS), t % SUBS
+            i, r = p * CORES + core, rows_of(s)
+
+            @pl.when(s == 0)
+            def _():
+                pair_copy(p).wait_recv()
+
             for j in range(n_node):
                 for h in range(2):
-                    spot = (j // lo_count, j % lo_count, h)
+                    spot = (j // lo_count, j % lo_count, h, r)
                     lev[(i,) + spot] = level(lev[(i,) + spot]) + level(pair[(p,) + spot])
-            for copy in first_copies(p):
+            for copy in first_copies(p, s):
                 copy.start()
 
-        @pl.when(t == 1)
+        @pl.when(t == SUBS)
         def _():
             p = piece(0)
             i = p * CORES + core
-            pair_copy(p).wait_recv()
             for flip in range(2):
                 for copy in raw_copies(flip):
                     copy.wait_recv()
@@ -237,42 +267,40 @@
             for j in range(2):
                 kept(0, j, (j, lo, 0))
                 kept(1, j, (hi, j, 1))
-            for copy in second_copies(p):
-                copy.start()
-
-        @pl.when((t >= 2) & (t <= n_z))
-        def _():
-            p = piece(t - 1)
-            i = p * CORES + core
-            for copy in first_copies(p):
+            for s in range(SUBS):
+                for copy in second_copies(p, s):
+                    copy.start()
+
+        @pl.when((t > SUBS) & (t <= items))
+        def _():
+            p, s = piece((t - 1) // SUBS), (t - 1) % SUBS
+            i, r = p * CORES + core, rows_of(s)
+            for copy in first_copies(p, s):
                 copy.wait_recv()
             for j in range(2):
-                lev[i, j, lo, 0] = lev[i, j, lo, 0] + first[p, 0, j]
-                lev[i, hi, j, 1] = lev[i, hi, j, 1] + first[p, 1, j]
-            for copy in second_copies(p):
+                lev[i, j, lo, 0, r] = lev[i, j, lo, 0, r] + first[p, 0, j, r]
+                lev[i, hi, j, 1, r] = lev[i, hi, j, 1, r] + first[p, 1, j, r]
+            for copy in second_copies(p, s):
                 copy.start()
 
-        @pl.when(t >= 2)
-        def _():
-            p = piece(t - 2)
-            i = p * CORES + core
-            for copy in second_copies(p):
-                copy.wait_recv()
-            for h in range(2):
-                lev[i, hi, lo, h] = lev[i, hi, lo, h] + second[p, h]
-
-            @pl.when(p != z)
-            def _():
-                third_copy(p, z).start()
+        @pl.when(t == SUBS + 1)
+        def _():
+            for s in range(SUBS):
+                last_exchange(piece(0), s)
+
+        @pl.when(t >= SUBS + 2)
+        def _():
+            last_exchange(piece((t - 2) // SUBS), (t - 2) % SUBS)
 
         return carry
 
-    lax.fori_loop(1, n_z + 2, pipeline, 0)
+    lax.fori_loop(SUBS, items + 2, pipeline, 0)
 
     total = lev[intra, hi, lo]
     for step in range(1, n_z):
         other = lax.rem(z + step, n_z)
-        third_copy(other, other).wait_recv()
+        for s in range(SUBS):
+            third_copy(other, other, s).wait_recv()
         total = total + third[other]
     for h in range(2):
         sum_ref[h * half : (h + 1) * half, :] = total[h]
@@ -288,17 +316,20 @@
     def finish(k, carry):
         p = piece(k)
         pair_copy(p).wait_send()
-        for copy in second_copies(p):
-            copy.wait_send()
+        for s in range(SUBS):
+            for copy in second_copies(p, s):
+                copy.wait_send()
 
         @pl.when(k > 0)
         def _():
-            for copy in first_copies(p):
-                copy.wait_send()
+            for s in range(SUBS):
+                for copy in first_copies(p, s):
+                    copy.wait_send()
 
         @pl.when(p != z)
         def _():
-            third_copy(p, z).wait_send()
+            for s in range(SUBS):
+                third_copy(p, z, s).wait_send()
 
         return carry
 
@@ -368,9 +399,9 @@
             dma((SLOTS,)),
             dma((n_z,)), dma((n_z,)),
             dma((2, 2)), dma((2, 2)),
-            dma((2, n_z)), dma((2, n_z)),
-            dma((2, n_z)), dma((2, n_z)),
-            dma((n_z,)), dma((n_z,)),
+            dma((2, n_z * SUBS)), dma((2, n_z * SUBS)),
+            dma((2, n_z * SUBS)), dma((2, n_z * SUBS)),
+            dma((n_z * SUBS,)), dma((n_z * SUBS,)),
             dma((group,)), dma((group,)),
             dma((n_z,)), dma((n_z,)),
         ],

time: 49 us -> 48.1 us (0.982)
  Pallas kernels: 46.8 us -> 45.9 us
    pallas_call x1, Pallas kernels: 44.4 us -> 43.5 us  [shards(): pl.pallas_call(functools.partial(reduce_kernel, n_node, n_intra), out_sha...]
where the time goes in v3:
time: 48.1 us; the launch traced here: 47.8 us
  Pallas kernels  45.9 us (95%)
  between operations  1.93 us (4%)
    pallas_call x1, Pallas kernels, shards(): pl.pallas_call(functools.partial(reduce_kernel, n_node, n_intra), out_sha...  43.5 us
    pallas_call x1, Pallas kernels, shards(): pl.pallas_call(functools.partial(adam_kernel, float(n_node * n_intra)), o...  2.4 us

profile of v3, /device:TPU:0, one launch (start us, length us, event | category | flops | bytes accessed | tf_op | source)
XLA Modules:
  0.0 47.8 jit_solution(6368029919895067464)
XLA Ops:
  1.9 43.5 %shard_map.94 = (f32[384,128]{1,0:T(8,128)}, f32[8,128]{1,0:T(8,128)}) custom-call(bf16[3072,512]{1,0:T(8,128)(2,1)} %bitcast.1, s32[64,512]{1,0:T(8,128)} %sign_ref.3), custom_call_target="tpu_custom_call" | custom-call | tf_op jit(solution)/shard_map/pallas_call | solution.py:380
  45.4 2.4 %shard_map.95 = (f32[384,128]{1,0:T(8,128)}, f32[384,128]{1,0:T(8,128)}, f32[384,128]{1,0:T(8,128)}) custom-call(f32[384,128]{1,0:T(8,128)} %get-tuple-element.5.sum_ref, f32[8,128]{1,0:T(8,128)} %get-tuple-element.6.top_ref, s32[64,512]{1,0:T(8,128)} %sign_ref.3, f32[1]{0:T(128)S(6)} %copy.10.scale_ref, s32[1]{0:T(128)S(6)} %copy.11.step_ref, ...), custom_call_target="tpu_custom_call" | custom-call | tf_op jit(solution)/shard_map/pallas_call | solution.py:413
